TPU v7x, 32 devices: a whole 2x2x4 slice. The times are simulated.
32 devices in a mesh: sub: 2 (over y), row: 4 (over x, core), col: 4 (over z).
Axes of the slice: x: 2, y: 2, z: 4, core: 2. Of those that a mesh axis runs over, the one named last changes fastest.
Arguments:
- factor_window: bfloat16 [2, 8192, 1024], P('sub', ('row', 'col'))
- right_sides: bfloat16 [2, 8192, 2048], P('sub', 'row', 'col'), may hold values from -1.1953125 to 1.1953125
- first_block: int32 [2, 8], P('sub'), may hold values from 0 to 4
- tile_map: int32 [2, 8], P('sub'), may hold values from 0 to 15, as said below
- interface_block: float32 [4096, 4096], P(('sub', 'row'), 'col'), may hold values from -6 to 6
Outputs:
- updated_sides: bfloat16 [2, 8192, 2048], P('sub', 'row', 'col')
- schur_global: float32 [4096, 4096], P(('sub', 'row'), 'col')
Inputs may be any that keep to these rules, and one draw needn't show every extreme that they name: `tile_map`: the 8 entries of a subdomain are different global tiles.
All inputs are finite; a program needn't handle non-finite values.
Results may differ from a plain program's by a relative error of at most 0.0075.
Values may be sent and summed in bfloat16 or wider, within the bound.
A program may use at most 64 MiB of HBM per device.

v0:
```python
import jax
import jax.numpy as jnp
from jax import lax
from jax.sharding import PartitionSpec as P

PANEL = 256
BLOCK = 256
STEPS = 4
GTILES = 16


def spread_2(value, axis, source):
    kept = jnp.where(lax.axis_index(axis) == source, value, 0).astype(value.dtype)
    return lax.psum(kept, axis)


def spread_tiles(columns, tile_map, block_count):
    onehot = (tile_map[0][:, None] == jnp.arange(GTILES, dtype=jnp.int32)[None, :]).astype(
        jnp.bfloat16
    )
    height = columns.shape[0]
    spread = jnp.einsum(
        "qbj,bg->qgj",
        columns.reshape(height, block_count, BLOCK),
        onehot,
        preferred_element_type=jnp.float32,
    )
    return spread.reshape(height, GTILES * BLOCK).astype(jnp.bfloat16)


def local(factor_window, right_sides, first_block, tile_map, interface_block):
    row_count = lax.axis_size("row")
    row_pos = lax.axis_index("row")
    col_pos = lax.axis_index("col")
    local_factor = factor_window[0]
    local_sides = right_sides[0]
    block_rows = local_sides.shape[0]
    block_cols = local_sides.shape[1]
    block_count = first_block.shape[1]
    row_global = row_pos * block_rows + jnp.arange(block_rows, dtype=jnp.int32)
    col_global = col_pos * block_cols + jnp.arange(block_cols, dtype=jnp.int32)
    col_block = col_global // BLOCK
    block_ids = jnp.arange(block_count, dtype=jnp.int32)
    first_col = jnp.sum(
        jnp.where(col_block[:, None] == block_ids[None, :], first_block[0][None, :], 0), axis=1
    )
    live = (row_global // PANEL)[:, None] >= first_col[None, :]
    current = jnp.where(live, local_sides.astype(jnp.float32), jnp.float32(0.0))
    is_root = row_pos == 0
    factor_rows = lax.all_gather(local_factor, "col", axis=0, tiled=True)
    pieces = []
    for panel in range(STEPS):
        offset = panel * PANEL
        panel_cols = factor_rows[:, offset : offset + PANEL]
        diag_block = panel_cols[offset : offset + PANEL].astype(jnp.float32)
        diag_block = jnp.where(is_root, diag_block, jnp.eye(PANEL, dtype=jnp.float32))
        solved = jax.scipy.linalg.solve_triangular(
            diag_block, current[offset : offset + PANEL], lower=True
        ).astype(jnp.bfloat16)
        solved = spread_2(solved, "row", 0)
        update = jnp.dot(panel_cols, solved, preferred_element_type=jnp.float32)
        current = jnp.where((row_global >= offset + PANEL)[:, None], current - update, current)
        placed = jnp.where(is_root, solved.astype(jnp.float32), current[offset : offset + PANEL])
        current = current.at[offset : offset + PANEL].set(placed)
        pieces.append(solved)
    updated_sides = current.astype(jnp.bfloat16)[None]
    stacked = jnp.concatenate(pieces, axis=0)
    out_cols = interface_block.shape[1]
    share = stacked.shape[0] // row_count
    my_share = lax.dynamic_slice_in_dim(stacked, row_pos * share, share, 0)
    all_columns = lax.all_gather(my_share, "col", axis=1, tiled=True)
    spread = spread_tiles(all_columns, tile_map, block_count)
    my_columns = lax.dynamic_slice_in_dim(spread, col_pos * out_cols, out_cols, 1)
    summed = lax.psum_scatter(
        lax.dot_general(
            spread, my_columns, (((0,), (0,)), ((), ())), preferred_element_type=jnp.float32
        ).astype(jnp.bfloat16),
        ("sub", "row"),
        scatter_dimension=0,
        tiled=True,
    ).astype(jnp.float32)
    schur_global = interface_block - summed
    return (updated_sides, schur_global)


def solution(mesh):
    return jax.shard_map(
        local,
        mesh=mesh,
        in_specs=(
            P("sub", ("row", "col"), None),
            P("sub", "row", "col"),
            P("sub", None),
            P("sub", None),
            P(("sub", "row"), "col"),
        ),
        out_specs=(P("sub", "row", "col"), P(("sub", "row"), "col")),
        check_vma=False,
    )
```

profile of v0, /device:TPU:0, one launch (start us, length us, event | category | flops | bytes accessed | tf_op | source)
XLA Modules:
  0.0 394.8 jit_solution(10873900418680429173)
XLA Ops:
  7.2 0.7 all-gather.6.cloned.1.call-update
  8.0 0.7 select_reduce_fusion
  8.8 3.5 convert_select_fusion
  12.3 80.8 %all-gather.6.cloned.1.call-done = bf16[1,2048,1024]{2,1,0:T(8,128)(2,1)} async-done(((bf16[1,512,1024]{2,1,0:T(8,128)(2,1)}), bf16[1,2048,1024]{2,1,0:T(8,128)(2,1)}) %all-gather.6.cloned.1.call-update) | async-done | bytes 4194320 | tf_op jit(solution)/shard_map/all_gather | solution.py:50
  93.0 1.2 fusion.16
  94.3 3.8 while.12
  94.4 0.6 fusion.72
  94.9 1.3 bitcast_dynamic-update-slice_fusion.8
  96.2 0.6 fusion.72
  96.8 1.3 bitcast_dynamic-update-slice_fusion.8
  98.1 19.7 %custom-call.6 = f32[2,128,128]{1,2,0:T(8,128)S(1)} custom-call(f32[2,128,128]{2,1,0:T(8,128)S(1)} %get-tuple-element.77), custom_call_target="InvertDiagBlocksLowerTriangular" | custom-call | tf_op jit(solution)/shard_map/jit(_solve_triangular)/triangular_solve | solution.py:57
  117.8 1.4 fusion.26
  119.2 1.3 convolution_subtract_fusion.3
  120.5 0.4 fusion.35
  120.9 0.7 fusion.12
  121.7 4.0 %while.13 = (s32[]{:T(128)}, f32[256,256]{1,0:T(8,128)S(1)}, s32[2,2]{1,0:T(2,128)S(1)}, f32[2,128,128]{2,1,0:T(8,128)S(1)}, s32[]{:T(128)}) while((s32[]{:T(128)}, f32[256,256]{1,0:T(8,128)S(1)}, s32[2,2]{1,0:T(2,128)S(1)}, f32[2,128,128]{2,1,0:T(8,128)S(1)}, s32[]{:T(128)}) %tuple.113), condition=%wide.while_cond.4.clone, body=%wide.while_body.4.clone.sunk | while | flops 2 | bytes 131181 | solution.py:57
  121.8 0.7 fusion.73
  122.4 1.3 bitcast_dynamic-update-slice_fusion.9
  123.8 0.7 fusion.73
  124.5 1.3 bitcast_dynamic-update-slice_fusion.9
  125.8 19.7 %custom-call.7 = f32[2,128,128]{1,2,0:T(8,128)S(1)} custom-call(f32[2,128,128]{2,1,0:T(8,128)S(1)} %get-tuple-element.78), custom_call_target="InvertDiagBlocksLowerTriangular" | custom-call | tf_op jit(solution)/shard_map/jit(_solve_triangular)/triangular_solve | solution.py:57
  145.5 7.4 %all-reduce.5.cloned.1.call-done = bf16[256,512]{1,0:T(8,128)(2,1)} async-done(((bf16[256,512]{1,0:T(8,128)(2,1)}), bf16[256,512]{1,0:T(8,128)(2,1)}) %all-reduce.5.cloned.1.call-update) | async-done | bytes 262160 | tf_op jit(solution)/shard_map/psum | solution.py:14
  152.9 3.4 subtract_select_fusion.3
  156.4 0.4 fusion.24
  156.8 1.6 copy-done.2
  158.4 0.4 convolution_subtract_fusion.2
  158.8 0.4 fusion.33
  159.2 0.7 fusion.11
  160.2 4.0 %while.14 = (s32[]{:T(128)}, f32[256,256]{1,0:T(8,128)S(1)}, s32[2,2]{1,0:T(2,128)S(1)}, f32[2,128,128]{2,1,0:T(8,128)S(1)}, s32[]{:T(128)}) while((s32[]{:T(128)}, f32[256,256]{1,0:T(8,128)S(1)}, s32[2,2]{1,0:T(2,128)S(1)}, f32[2,128,128]{2,1,0:T(8,128)S(1)}, s32[]{:T(128)}) %tuple.114), condition=%wide.while_cond.4.clone.1, body=%wide.while_body.4.clone.1.sunk | while | flops 2 | bytes 131181 | solution.py:57
  160.2 0.6 fusion.74
  160.8 1.4 bitcast_dynamic-update-slice_fusion.10
  162.2 0.6 fusion.74
  162.8 1.4 bitcast_dynamic-update-slice_fusion.10
  164.2 19.7 %custom-call.8 = f32[2,128,128]{1,2,0:T(8,128)S(1)} custom-call(f32[2,128,128]{2,1,0:T(8,128)S(1)} %get-tuple-element.79), custom_call_target="InvertDiagBlocksLowerTriangular" | custom-call | tf_op jit(solution)/shard_map/jit(_solve_triangular)/triangular_solve | solution.py:57
  183.9 8.8 %all-reduce.7.cloned.1.call-done = bf16[256,512]{1,0:T(8,128)(2,1)} async-done(((bf16[256,512]{1,0:T(8,128)(2,1)}), bf16[256,512]{1,0:T(8,128)(2,1)}) %all-reduce.7.cloned.1.call-update) | async-done | bytes 262160 | tf_op jit(solution)/shard_map/psum | solution.py:14
  192.7 3.4 subtract_select_fusion.2
  196.2 0.4 fusion.22
  196.7 1.6 copy-done.1
  198.2 0.4 convolution_subtract_fusion.1
  198.6 0.4 fusion.31
  199.0 0.7 fusion.10
  199.9 3.8 while.15
  199.9 0.6 fusion.75
  200.5 1.3 bitcast_dynamic-update-slice_fusion.11
  201.8 0.6 fusion.75
  202.4 1.3 bitcast_dynamic-update-slice_fusion.11
  203.7 19.7 %custom-call.9 = f32[2,128,128]{1,2,0:T(8,128)S(1)} custom-call(f32[2,128,128]{2,1,0:T(8,128)S(1)} %get-tuple-element.80), custom_call_target="InvertDiagBlocksLowerTriangular" | custom-call | tf_op jit(solution)/shard_map/jit(_solve_triangular)/triangular_solve | solution.py:57
  223.4 9.2 %all-reduce.9.cloned.1.call-done = bf16[256,512]{1,0:T(8,128)(2,1)} async-done(((bf16[256,512]{1,0:T(8,128)(2,1)}), bf16[256,512]{1,0:T(8,128)(2,1)}) %all-reduce.9.cloned.1.call-update) | async-done | bytes 262160 | tf_op jit(solution)/shard_map/psum | solution.py:14
  232.5 3.4 subtract_select_fusion.1
  236.0 0.4 fusion.20
  236.5 1.6 copy-done
  238.0 0.4 convolution_subtract_fusion
  238.4 0.4 fusion.29
  238.8 0.7 fusion.9
  239.7 32.3 %all-reduce.11.cloned.1.call-done = bf16[256,512]{1,0:T(8,128)(2,1)} async-done(((bf16[256,512]{1,0:T(8,128)(2,1)}), bf16[256,512]{1,0:T(8,128)(2,1)}) %all-reduce.11.cloned.1.call-update) | async-done | bytes 262160 | tf_op jit(solution)/shard_map/psum | solution.py:14
  272.0 3.4 subtract_select_fusion
  275.4 1.6 fusion.19
  277.2 27.9 %all-gather.4.cloned.1.call-done = bf16[256,2048]{1,0:T(8,128)(2,1)} async-done(((bf16[256,512]{1,0:T(8,128)(2,1)}), bf16[256,2048]{1,0:T(8,128)(2,1)}) %all-gather.4.cloned.1.call-update) | async-done | bytes 1048592 | tf_op jit(solution)/shard_map/all_gather | solution.py:71
  305.1 1.5 copy.19
  306.7 0.8 convolution_convert_fusion.1
  307.5 0.9 copy.20
  308.4 5.6 %convolution_convert_fusion = bf16[4096,1024]{1,0:T(8,128)(2,1)} fusion(bf16[256,4096]{1,0:T(8,128)(2,1)S(1)} %bitcast.105, s32[]{:T(128)S(6)} %select_n.126), kind=kOutput, calls=%fused_computation.8 | convolution fusion | flops 2151677952 | bytes 11010052 | tf_op jit(solution)/shard_map/dot_general | solution.py:75
  314.1 71.0 %reduce-scatter.2.cloned.1.call-done = bf16[512,1024]{1,0:T(8,128)(2,1)} async-done(((bf16[4096,1024]{1,0:T(8,128)(2,1)}), bf16[512,1024]{1,0:T(8,128)(2,1)}) %reduce-scatter.2.cloned.1.call-update) | async-done | bytes 1048592 | tf_op jit(solution)/shard_map/reduce_scatter | solution.py:74
  385.1 2.8 convert_subtract_fusion
  (55 shorter events, 1.4 us)
Async XLA Ops:
  7.2 85.9 %all-gather.6.cloned.1.call-start = ((), (), s32[]{:S(2)}) async-start(), calls=%async_computation.7 | async-start | bytes 5242880 | tf_op jit(solution)/shard_map/all_gather | solution.py:50
  7.9 145.0 %all-reduce.5.cloned.1.call-start = ((), (), s32[]{:S(2)}) async-start(), calls=%async_computation.1 | async-start | bytes 524288 | tf_op jit(solution)/shard_map/psum | solution.py:14
  12.3 140.6 %copy-start.6 = (bf16[1,2048,512]{2,1,0:T(8,128)(2,1)S(1)}, bf16[1,2048,512]{2,1,0:T(8,128)(2,1)}, u32[]{:S(2)}) copy-start(bf16[1,2048,512]{2,1,0:T(8,128)(2,1)} %param.16) | copy-start | bytes 6291460
  121.7 71.0 %all-reduce.7.cloned.1.call-start = ((), (), s32[]{:S(2)}) async-start(), calls=%async_computation.2 | async-start | bytes 524288 | tf_op jit(solution)/shard_map/psum | solution.py:14
  152.9 3.4 copy-start.8
  156.4 2.0 copy-start.2
  160.0 72.6 %all-reduce.9.cloned.1.call-start = ((), (), s32[]{:S(2)}) async-start(), calls=%async_computation.3 | async-start | bytes 524288 | tf_op jit(solution)/shard_map/psum | solution.py:14
  192.7 3.4 copy-start.4
  196.2 2.0 copy-start.1
  199.8 72.2 %all-reduce.11.cloned.1.call-start = ((), (), s32[]{:S(2)}) async-start(), calls=%async_computation.4 | async-start | bytes 524288 | tf_op jit(solution)/shard_map/psum | solution.py:14
  232.5 3.4 copy-start.5
  236.0 2.0 copy-start
  239.6 65.5 %all-gather.4.cloned.1.call-start = ((), (), s32[]{:S(2)}) async-start(), calls=%async_computation.5 | async-start | bytes 1310720 | tf_op jit(solution)/shard_map/all_gather | solution.py:71
  239.7 67.0 %copy-start.10 = (s32[1,8]{1,0:T(1,128)S(1)}, s32[1,8]{1,0:T(1,128)}, u32[]{:S(2)}) copy-start(s32[1,8]{1,0:T(1,128)} %param.18) | copy-start | bytes 100
  272.0 3.4 copy-start.9
  276.9 31.5 %copy-start.3 = (bf16[2048,512]{1,0:T(8,128)(2,1)}, bf16[2048,512]{1,0:T(8,128)(2,1)S(1)}, u32[]{:S(2)}) copy-start(bf16[2048,512]{1,0:T(8,128)(2,1)S(1)} %get-tuple-element.126) | copy-start | bytes 6291460
  277.0 108.2 %reduce-scatter.2.cloned.1.call-start = ((), (), s32[]{:S(2)}) async-start(), calls=%async_computation.6 | async-start | bytes 9437184 | tf_op jit(solution)/shard_map/reduce_scatter | solution.py:74
  314.1 71.1 %copy-start.7 = (f32[512,1024]{1,0:T(8,128)S(1)}, f32[512,1024]{1,0:T(8,128)}, u32[]{:S(2)}) copy-start(f32[512,1024]{1,0:T(8,128)} %param.19) | copy-start | bytes 6291460
Sparse Core Ops, SparseCore 0:
  9.5 83.4 all-gather.5
  121.8 31.0 all-reduce.4
  160.1 32.5 all-reduce.6
  199.9 32.5 all-reduce.8
  239.7 32.2 all-reduce.10
  277.1 27.9 all-gather.3
  314.2 70.8 reduce-scatter.1
where the time goes:
time: 395 us
  waiting for transfers between devices  238 us (60%)
  other arithmetic  92 us (23%)
  matrix products  26.7 us (7%)
  local copies, waits for them, and re-layouts  22.7 us (6%)
  between operations  14.5 us (4%)
    all_gather x1, waiting for transfers between devices, local(): factor_rows = lax.all_gather(local_factor, 'col', axis=0, tiled=True)  80.8 us
    another operation x6, other arithmetic, local(): jax.scipy.linalg.solve_triangular(diag_block, current[offset:offset + PAN...  79.9 us
    reduce_scatter x1, waiting for transfers between devices, local(): lax.psum_scatter(lax.dot_general(spread, my_columns, (((0,), (0,)), ((),...  71 us
    psum x4, waiting for transfers between devices, spread_2(): return lax.psum(kept, axis)  57.7 us
    all_gather x1, waiting for transfers between devices, local(): all_columns = lax.all_gather(my_share, 'col', axis=1, tiled=True)  27.9 us
    another operation x29, local copies, waits for them, and re-layouts, local(): jax.scipy.linalg.solve_triangular(diag_block, current[offset:offset + PAN...  15.5 us
    dot_general x4, matrix products, local(): update = jnp.dot(panel_cols, solved, preferred_element_type=jnp.float32)  13.4 us
  transfers between devices with their start and end apart: 7, of which 7 were waited for; matrix products, arithmetic and copies ran while one was open for 19% of the time, Pallas kernels for 0%

commit v1 on v0

--- a/solution.py
+++ b/solution.py
@@ -68,7 +68,12 @@
     out_cols = interface_block.shape[1]
     share = stacked.shape[0] // row_count
     my_share = lax.dynamic_slice_in_dim(stacked, row_pos * share, share, 0)
-    all_columns = lax.all_gather(my_share, "col", axis=1, tiled=True)
+    ring = [my_share]
+    for hop in range(3):
+        ring.append(lax.ppermute(ring[-1], "col", [(dev, (dev + 1) % 4) for dev in range(4)]))
+    all_columns = jnp.roll(
+        jnp.concatenate(ring[::-1], axis=1), (lax.axis_index("col") + 1) * ring[0].shape[1], axis=1
+    )
     spread = spread_tiles(all_columns, tile_map, block_count)
     my_columns = lax.dynamic_slice_in_dim(spread, col_pos * out_cols, out_cols, 1)
     summed = lax.psum_scatter(

time: 395 us -> 389 us (0.985)
  waiting for transfers between devices: 238 us -> 232 us
    all_gather x1 -> x0, waiting for transfers between devices: 27.9 us -> none  [local(): all_columns = lax.all_gather(my_share, 'col', axis=1, tiled=True)]
    ppermute x0 -> x3, waiting for transfers between devices: none -> 23.3 us  [local(): lax.ppermute(ring[-1], 'col', [(dev, (dev + 1) % 4) for dev in range(4)])]
  transfers between devices with their start and end apart: 7 -> 9, of which waited for: 7 -> 9; matrix products, arithmetic and copies ran while one was open for 19% -> 19% of each run, Pallas kernels for 0% -> 0%
where the time goes in v1:
time: 389 us
  waiting for transfers between devices  232 us (60%)
  other arithmetic  91.3 us (23%)
  matrix products  26.7 us (7%)
  local copies, waits for them, and re-layouts  21.7 us (6%)
  between operations  14.6 us (4%)
    all_gather x1, waiting for transfers between devices, local(): factor_rows = lax.all_gather(local_factor, 'col', axis=0, tiled=True)  80.8 us
    another operation x6, other arithmetic, local(): jax.scipy.linalg.solve_triangular(diag_block, current[offset:offset + PAN...  79.9 us
    reduce_scatter x1, waiting for transfers between devices, local(): lax.psum_scatter(lax.dot_general(spread, my_columns, (((0,), (0,)), ((),...  69.9 us
    psum x4, waiting for transfers between devices, spread_2(): return lax.psum(kept, axis)  57.7 us
    ppermute x3, waiting for transfers between devices, local(): lax.ppermute(ring[-1], 'col', [(dev, (dev + 1) % 4) for dev in range(4)])  23.3 us
    another operation x29, local copies, waits for them, and re-layouts, local(): jax.scipy.linalg.solve_triangular(diag_block, current[offset:offset + PAN...  15.5 us
    dot_general x4, matrix products, local(): update = jnp.dot(panel_cols, solved, preferred_element_type=jnp.float32)  13.4 us
  transfers between devices with their start and end apart: 9, of which 9 were waited for; matrix products, arithmetic and copies ran while one was open for 19% of the time, Pallas kernels for 0%

profile of v1, /device:TPU:0, one launch (start us, length us, event | category | flops | bytes accessed | tf_op | source)
XLA Modules:
  0.0 388.9 jit_solution(10532520779711605961)
XLA Ops:
  7.2 0.7 all-gather.3.cloned.1.call-update
  8.0 0.7 select_reduce_fusion
  8.8 3.5 convert_select_fusion
  12.3 80.8 %all-gather.3.cloned.1.call-done = bf16[1,2048,1024]{2,1,0:T(8,128)(2,1)} async-done(((bf16[1,512,1024]{2,1,0:T(8,128)(2,1)}), bf16[1,2048,1024]{2,1,0:T(8,128)(2,1)}) %all-gather.3.cloned.1.call-update) | async-done | bytes 4194320 | tf_op jit(solution)/shard_map/all_gather | solution.py:50
  93.0 1.2 fusion.16
  94.3 3.8 while.12
  94.4 0.6 fusion.72
  94.9 1.3 bitcast_dynamic-update-slice_fusion.8
  96.2 0.6 fusion.72
  96.8 1.3 bitcast_dynamic-update-slice_fusion.8
  98.1 19.7 %custom-call.6 = f32[2,128,128]{1,2,0:T(8,128)S(1)} custom-call(f32[2,128,128]{2,1,0:T(8,128)S(1)} %get-tuple-element.77), custom_call_target="InvertDiagBlocksLowerTriangular" | custom-call | tf_op jit(solution)/shard_map/jit(_solve_triangular)/triangular_solve | solution.py:57
  117.8 1.4 fusion.26
  119.2 1.3 convolution_subtract_fusion.3
  120.5 0.4 fusion.35
  120.9 0.7 fusion.12
  121.7 4.0 %while.13 = (s32[]{:T(128)}, f32[256,256]{1,0:T(8,128)S(1)}, s32[2,2]{1,0:T(2,128)S(1)}, f32[2,128,128]{2,1,0:T(8,128)S(1)}, s32[]{:T(128)}) while((s32[]{:T(128)}, f32[256,256]{1,0:T(8,128)S(1)}, s32[2,2]{1,0:T(2,128)S(1)}, f32[2,128,128]{2,1,0:T(8,128)S(1)}, s32[]{:T(128)}) %tuple.111), condition=%wide.while_cond.4.clone, body=%wide.while_body.4.clone.sunk | while | flops 2 | bytes 131181 | solution.py:57
  121.8 0.7 fusion.73
  122.4 1.3 bitcast_dynamic-update-slice_fusion.9
  123.8 0.7 fusion.73
  124.5 1.3 bitcast_dynamic-update-slice_fusion.9
  125.8 19.7 %custom-call.7 = f32[2,128,128]{1,2,0:T(8,128)S(1)} custom-call(f32[2,128,128]{2,1,0:T(8,128)S(1)} %get-tuple-element.78), custom_call_target="InvertDiagBlocksLowerTriangular" | custom-call | tf_op jit(solution)/shard_map/jit(_solve_triangular)/triangular_solve | solution.py:57
  145.5 7.4 %all-reduce.5.cloned.1.call-done = bf16[256,512]{1,0:T(8,128)(2,1)} async-done(((bf16[256,512]{1,0:T(8,128)(2,1)}), bf16[256,512]{1,0:T(8,128)(2,1)}) %all-reduce.5.cloned.1.call-update) | async-done | bytes 262160 | tf_op jit(solution)/shard_map/psum | solution.py:14
  152.9 3.4 subtract_select_fusion.3
  156.4 0.4 fusion.24
  156.8 1.6 copy-done.2
  158.4 0.4 convolution_subtract_fusion.2
  158.8 0.4 fusion.33
  159.2 0.7 fusion.11
  160.2 4.0 %while.14 = (s32[]{:T(128)}, f32[256,256]{1,0:T(8,128)S(1)}, s32[2,2]{1,0:T(2,128)S(1)}, f32[2,128,128]{2,1,0:T(8,128)S(1)}, s32[]{:T(128)}) while((s32[]{:T(128)}, f32[256,256]{1,0:T(8,128)S(1)}, s32[2,2]{1,0:T(2,128)S(1)}, f32[2,128,128]{2,1,0:T(8,128)S(1)}, s32[]{:T(128)}) %tuple.112), condition=%wide.while_cond.4.clone.1, body=%wide.while_body.4.clone.1.sunk | while | flops 2 | bytes 131181 | solution.py:57
  160.2 0.6 fusion.74
  160.8 1.4 bitcast_dynamic-update-slice_fusion.10
  162.2 0.6 fusion.74
  162.8 1.4 bitcast_dynamic-update-slice_fusion.10
  164.2 19.7 %custom-call.8 = f32[2,128,128]{1,2,0:T(8,128)S(1)} custom-call(f32[2,128,128]{2,1,0:T(8,128)S(1)} %get-tuple-element.79), custom_call_target="InvertDiagBlocksLowerTriangular" | custom-call | tf_op jit(solution)/shard_map/jit(_solve_triangular)/triangular_solve | solution.py:57
  183.9 8.8 %all-reduce.7.cloned.1.call-done = bf16[256,512]{1,0:T(8,128)(2,1)} async-done(((bf16[256,512]{1,0:T(8,128)(2,1)}), bf16[256,512]{1,0:T(8,128)(2,1)}) %all-reduce.7.cloned.1.call-update) | async-done | bytes 262160 | tf_op jit(solution)/shard_map/psum | solution.py:14
  192.7 3.4 subtract_select_fusion.2
  196.2 0.4 fusion.22
  196.7 1.6 copy-done.1
  198.6 0.4 fusion.31
  199.0 0.7 fusion.10
  199.9 3.8 while.15
  199.9 0.6 fusion.75
  200.5 1.3 bitcast_dynamic-update-slice_fusion.11
  201.8 0.6 fusion.75
  202.4 1.3 bitcast_dynamic-update-slice_fusion.11
  203.7 19.7 %custom-call.9 = f32[2,128,128]{1,2,0:T(8,128)S(1)} custom-call(f32[2,128,128]{2,1,0:T(8,128)S(1)} %get-tuple-element.80), custom_call_target="InvertDiagBlocksLowerTriangular" | custom-call | tf_op jit(solution)/shard_map/jit(_solve_triangular)/triangular_solve | solution.py:57
  223.4 9.2 %all-reduce.9.cloned.1.call-done = bf16[256,512]{1,0:T(8,128)(2,1)} async-done(((bf16[256,512]{1,0:T(8,128)(2,1)}), bf16[256,512]{1,0:T(8,128)(2,1)}) %all-reduce.9.cloned.1.call-update) | async-done | bytes 262160 | tf_op jit(solution)/shard_map/psum | solution.py:14
  232.5 3.4 subtract_select_fusion.1
  236.0 0.4 fusion.20
  236.5 1.6 copy-done
  238.4 0.4 fusion.29
  238.8 0.7 fusion.9
  239.7 32.3 %all-reduce.11.cloned.1.call-done = bf16[256,512]{1,0:T(8,128)(2,1)} async-done(((bf16[256,512]{1,0:T(8,128)(2,1)}), bf16[256,512]{1,0:T(8,128)(2,1)}) %all-reduce.11.cloned.1.call-update) | async-done | bytes 262160 | tf_op jit(solution)/shard_map/psum | solution.py:14
  272.0 3.4 subtract_select_fusion
  275.4 0.9 fusion.19
  276.3 1.5 collective-permute-start
  277.8 7.0 %collective-permute-done = bf16[256,512]{1,0:T(8,128)(2,1)S(1)} collective-permute-done((bf16[256,512]{1,0:T(8,128)(2,1)S(1)}, bf16[256,512]{1,0:T(8,128)(2,1)S(1)}, u32[]{:S(2)}, u32[]{:S(2)}) %collective-permute-start) | collective-permute-done | bytes 262176 | tf_op jit(solution)/shard_map/ppermute | solution.py:73
  284.8 8.2 %collective-permute-done.1 = bf16[256,512]{1,0:T(8,128)(2,1)S(1)} collective-permute-done((bf16[256,512]{1,0:T(8,128)(2,1)S(1)}, bf16[256,512]{1,0:T(8,128)(2,1)S(1)}, u32[]{:S(2)}, u32[]{:S(2)}) %collective-permute-start.1) | collective-permute-done | bytes 262176 | tf_op jit(solution)/shard_map/ppermute | solution.py:73
  293.0 8.2 %collective-permute-done.2 = bf16[256,512]{1,0:T(8,128)(2,1)S(1)} collective-permute-done((bf16[256,512]{1,0:T(8,128)(2,1)S(1)}, bf16[256,512]{1,0:T(8,128)(2,1)S(1)}, u32[]{:S(2)}, u32[]{:S(2)}) %collective-permute-start.2) | collective-permute-done | bytes 262176 | tf_op jit(solution)/shard_map/ppermute | solution.py:73
  301.8 0.8 convolution_convert_fusion.1
  302.6 0.9 copy.20
  303.6 5.6 %convolution_convert_fusion = bf16[4096,1024]{1,0:T(8,128)(2,1)} fusion(bf16[256,4096]{1,0:T(8,128)(2,1)S(1)} %bitcast.105, s32[]{:T(128)S(6)} %select_n.141), kind=kOutput, calls=%fused_computation.8 | convolution fusion | flops 2151677952 | bytes 11010052 | tf_op jit(solution)/shard_map/dot_general | solution.py:80
  309.3 69.9 %reduce-scatter.2.cloned.1.call-done = bf16[512,1024]{1,0:T(8,128)(2,1)} async-done(((bf16[4096,1024]{1,0:T(8,128)(2,1)}), bf16[512,1024]{1,0:T(8,128)(2,1)}) %reduce-scatter.2.cloned.1.call-update) | async-done | bytes 1048592 | tf_op jit(solution)/shard_map/reduce_scatter | solution.py:79
  379.2 2.8 convert_subtract_fusion
  (67 shorter events, 2.5 us)
Async XLA Ops:
  7.2 85.9 %all-gather.3.cloned.1.call-start = ((), (), s32[]{:S(2)}) async-start(), calls=%async_computation.6 | async-start | bytes 5242880 | tf_op jit(solution)/shard_map/all_gather | solution.py:50
  7.9 145.0 %all-reduce.5.cloned.1.call-start = ((), (), s32[]{:S(2)}) async-start(), calls=%async_computation.1 | async-start | bytes 524288 | tf_op jit(solution)/shard_map/psum | solution.py:14
  12.3 140.6 %copy-start.6 = (bf16[1,2048,512]{2,1,0:T(8,128)(2,1)S(1)}, bf16[1,2048,512]{2,1,0:T(8,128)(2,1)}, u32[]{:S(2)}) copy-start(bf16[1,2048,512]{2,1,0:T(8,128)(2,1)} %param.16) | copy-start | bytes 6291460
  121.7 71.0 %all-reduce.7.cloned.1.call-start = ((), (), s32[]{:S(2)}) async-start(), calls=%async_computation.2 | async-start | bytes 524288 | tf_op jit(solution)/shard_map/psum | solution.py:14
  152.9 3.4 copy-start.8
  156.4 2.0 copy-start.2
  160.0 72.6 %all-reduce.9.cloned.1.call-start = ((), (), s32[]{:S(2)}) async-start(), calls=%async_computation.3 | async-start | bytes 524288 | tf_op jit(solution)/shard_map/psum | solution.py:14
  192.7 3.4 copy-start.4
  196.2 2.0 copy-start.1
  199.8 72.2 %all-reduce.11.cloned.1.call-start = ((), (), s32[]{:S(2)}) async-start(), calls=%async_computation.4 | async-start | bytes 524288 | tf_op jit(solution)/shard_map/psum | solution.py:14
  232.5 3.4 copy-start.5
  236.0 2.0 copy-start
  239.6 139.6 %reduce-scatter.2.cloned.1.call-start = ((), (), s32[]{:S(2)}) async-start(), calls=%async_computation.5 | async-start | bytes 9437184 | tf_op jit(solution)/shard_map/reduce_scatter | solution.py:79
  272.0 3.4 copy-start.9
  276.3 25.6 %copy-start.3 = (bf16[2048,512]{1,0:T(8,128)(2,1)}, bf16[2048,512]{1,0:T(8,128)(2,1)S(1)}, u32[]{:S(2)}) copy-start(bf16[2048,512]{1,0:T(8,128)(2,1)S(1)} %get-tuple-element.126) | copy-start | bytes 6291460
  276.3 8.5 %collective-permute-start = (bf16[256,512]{1,0:T(8,128)(2,1)S(1)}, bf16[256,512]{1,0:T(8,128)(2,1)S(1)}, u32[]{:S(2)}, u32[]{:S(2)}) collective-permute-start(bf16[256,512]{1,0:T(8,128)(2,1)S(1)} %get-tuple-element.125), channel_id=1, source_target_pairs={{0,1},{1,2},{2,3},{3,0},{4,5},{5,6},{6,7},{7,4},{8,9},{9,10},{10,1... | collective-permute-start | bytes 786440 | tf_op jit(solution)/shard_map/ppermute | solution.py:73
  284.8 8.2 %collective-permute-start.1 = (bf16[256,512]{1,0:T(8,128)(2,1)S(1)}, bf16[256,512]{1,0:T(8,128)(2,1)S(1)}, u32[]{:S(2)}, u32[]{:S(2)}) collective-permute-start(bf16[256,512]{1,0:T(8,128)(2,1)S(1)} %collective-permute-done), channel_id=1, source_target_pairs={{0,1},{1,2},{2,3},{3,0},{4,5},{5,6},{6,7},{7,4},{8,9},{9,10},{10,1... | collective-permute-start | bytes 786440 | tf_op jit(solution)/shard_map/ppermute | solution.py:73
  293.0 8.2 %collective-permute-start.2 = (bf16[256,512]{1,0:T(8,128)(2,1)S(1)}, bf16[256,512]{1,0:T(8,128)(2,1)S(1)}, u32[]{:S(2)}, u32[]{:S(2)}) collective-permute-start(bf16[256,512]{1,0:T(8,128)(2,1)S(1)} %collective-permute-done.1), channel_id=1, source_target_pairs={{0,1},{1,2},{2,3},{3,0},{4,5},{5,6},{6,7},{7,4},{8,9},{9,10},{10,1... | collective-permute-start | bytes 786440 | tf_op jit(solution)/shard_map/ppermute | solution.py:73
  293.0 8.9 %copy-start.10 = (s32[1,8]{1,0:T(1,128)S(1)}, s32[1,8]{1,0:T(1,128)}, u32[]{:S(2)}) copy-start(s32[1,8]{1,0:T(1,128)} %param.18) | copy-start | bytes 100
  309.2 70.0 %copy-start.7 = (f32[512,1024]{1,0:T(8,128)S(1)}, f32[512,1024]{1,0:T(8,128)}, u32[]{:S(2)}) copy-start(f32[512,1024]{1,0:T(8,128)} %param.19) | copy-start | bytes 6291460
Sparse Core Ops, SparseCore 0:
  9.5 83.4 all-gather.2
  121.8 31.0 all-reduce.4
  160.1 32.5 all-reduce.6
  199.9 32.5 all-reduce.8
  239.7 32.2 all-reduce.10
  309.4 69.7 reduce-scatter.1
